TPU v7x, 32 devices: a whole 2x2x4 slice. The times are simulated.
32 devices in a mesh: rep: 32 (over z, y, x, core).
Axes of the slice: x: 2, y: 2, z: 4, core: 2. Of those that a mesh axis runs over, the one named last changes fastest.
Arguments:
- inputs: bfloat16 [16384, 1024], P('rep'), may hold values from -6 to 6
- out_grads: bfloat16 [16384, 4096], P('rep'), may hold values from -0.29882812 to 0.29882812
- error_in: bfloat16 [32, 1024, 4096], P('rep'), may hold values from -6 to 6
- q_start: float32 [32, 4096], replicated, may hold values from -0.09375 to 0.09375
- master: float32 [1024, 4096], P(None, 'rep'), may hold values from -1.2 to 1.2
Outputs:
- error_out: bfloat16 [32, 1024, 4096], P('rep')
- q_out: float32 [32, 4096], replicated
- master_out: float32 [1024, 4096], P(None, 'rep')
All inputs are finite; a program needn't handle non-finite values.
Results may differ from a plain program's by a relative error of at most 0.001.
Values sent between devices are 32-bit elements; how exact they have to be, the bound alone decides.
No kernel may reach another device: no remote copies, remote signals or barrier semaphores. Data moves between devices by JAX's collectives and lax.ppermute only.
A program may use at most 128 MiB of HBM per device.

v0:
```python
import jax
import jax.numpy as jnp
from jax import lax
from jax.sharding import PartitionSpec as P

ITERS = 3


def orthonormal(rows):
    basis = jnp.zeros_like(rows)
    for k in range(rows.shape[0]):
        vector = rows[k]
        coef = jnp.dot(basis, vector, precision=lax.Precision.HIGHEST)
        vector = vector - jnp.dot(coef, basis, precision=lax.Precision.HIGHEST)
        basis = basis.at[k].set(vector / jnp.sqrt(jnp.sum(vector * vector) + 1.0))
    return basis


def outer_rows(left, right):
    return lax.dot_general(
        left,
        right,
        (((0,), (0,)), ((), ())),
        precision=lax.Precision.HIGHEST,
        preferred_element_type=jnp.float32,
    )


def shards(inputs, out_grads, error_in, q_start, master):
    count = lax.axis_size("rep")
    grad = lax.dot_general(
        inputs, out_grads, (((0,), (0,)), ((), ())), preferred_element_type=jnp.float32
    )
    merged = grad + error_in[0].astype(jnp.float32)
    factor = q_start
    basis = None
    local_q = None
    for step in range(ITERS):
        local_p = lax.dot_general(
            factor,
            merged,
            (((1,), (1,)), ((), ())),
            precision=lax.Precision.HIGHEST,
            preferred_element_type=jnp.float32,
        )
        total_p = lax.psum(local_p, "rep")
        basis = orthonormal(total_p)
        local_q = jnp.dot(
            basis, merged, precision=lax.Precision.HIGHEST, preferred_element_type=jnp.float32
        )
        if step + 1 < ITERS:
            factor = lax.psum(local_q, "rep") / count
    width = master.shape[1]
    factor = lax.psum(local_q, "rep") / count
    recon = outer_rows(basis, factor)
    own_cols = lax.dynamic_slice_in_dim(recon, lax.axis_index("rep") * width, width, 1)
    master_out = master - 0.5 * own_cols
    error_out = (merged - recon).astype(jnp.bfloat16)[None]
    return (error_out, factor, master_out)


def solution(mesh):
    return jax.shard_map(
        shards,
        mesh=mesh,
        in_specs=(P("rep", None), P("rep", None), P("rep", None, None), P(), P(None, "rep")),
        out_specs=(P("rep", None, None), P(), P(None, "rep")),
        check_vma=False,
    )
```

profile of v0, /device:TPU:0, one launch (start us, length us, event | category | flops | bytes accessed | tf_op | source)
XLA Modules:
  0.0 1167.3 jit_solution(7776026956208568537)
XLA Ops:
  7.2 1.2 copy-done
  8.4 8.8 convert_add_fusion
  17.2 5.7 copy-done.1
  22.9 16.0 %convolution_bitcast_fusion = f32[32,1024]{1,0:T(8,128)} fusion(f32[1024,4096]{1,0:T(8,128)S(1)} %convert_add_fusion, f32[32,4096]{1,0:T(8,128)S(1)} %copy-done.3), kind=kOutput, calls=%fused_computation.3 | convolution fusion | flops 1610612736 | bytes 17432576 | tf_op jit(solution)/shard_map/dot_general | solution.py:39
  39.1 127.2 %all-reduce.10.cloned.1.call-done = f32[32,1024]{1,0:T(8,128)} async-done(((f32[32,1024]{1,0:T(8,128)}), f32[32,1024]{1,0:T(8,128)}) %all-reduce.10.cloned.1.call-update) | async-done | bytes 131088 | tf_op jit(solution)/shard_map/psum | solution.py:46
  167.4 1.2 fusion.236
  172.4 0.9 convolution_bitcast_fusion.94
  175.0 0.9 convolution_bitcast_fusion.93
  180.2 0.9 convolution_bitcast_fusion.91
  185.4 0.9 convolution_bitcast_fusion.89
  190.5 0.9 convolution_bitcast_fusion.87
  195.7 0.9 convolution_bitcast_fusion.85
  198.3 0.9 convolution_bitcast_fusion.84
  200.9 0.9 convolution_bitcast_fusion.83
  202.1 1.3 fusion.235
  204.8 0.9 convolution_bitcast_fusion.82
  212.6 0.9 convolution_bitcast_fusion.79
  217.8 0.9 convolution_bitcast_fusion.77
  220.3 0.9 convolution_bitcast_fusion.76
  222.9 0.9 convolution_bitcast_fusion.75
  228.1 0.9 convolution_bitcast_fusion.73
  233.3 0.9 convolution_bitcast_fusion.71
  235.9 0.9 convolution_bitcast_fusion.70
  238.5 0.9 convolution_bitcast_fusion.69
  241.0 0.9 convolution_bitcast_fusion.68
  246.2 0.9 convolution_bitcast_fusion.66
  248.8 0.9 convolution_bitcast_fusion.65
  251.6 13.9 %fusion.267 = f32[32,4096]{1,0:T(8,128)} fusion(f32[32,1024]{1,0:T(8,128)S(1)} %scatter.371, f32[1024,4096]{1,0:T(8,128)} %copy-done.1), kind=kOutput, calls=%fused_computation.560 | convolution fusion | flops 1610612736 | bytes 17432576 | tf_op jit(solution)/shard_map/dot_general | solution.py:48
  265.6 128.2 %all-reduce.12.cloned.1.call-done = f32[32,4096]{1,0:T(8,128)} async-done(((f32[32,4096]{1,0:T(8,128)}), f32[32,4096]{1,0:T(8,128)}) %all-reduce.12.cloned.1.call-update) | async-done | bytes 524304 | tf_op jit(solution)/shard_map/psum | solution.py:52
  393.8 19.3 %fusion.3 = f32[32,1024]{1,0:T(8,128)} fusion(f32[1024,4096]{1,0:T(8,128)} %copy-done.1, f32[32,4096]{1,0:T(8,128)} %all-reduce.12.cloned.1.call-done), kind=kOutput, calls=%fused_computation.103 | convolution fusion | flops 1610743808 | bytes 17432576 | tf_op jit(solution)/shard_map/dot_general | solution.py:39
  413.2 123.6 %all-reduce.14.cloned.1.call-done = f32[32,1024]{1,0:T(8,128)} async-done(((f32[32,1024]{1,0:T(8,128)}), f32[32,1024]{1,0:T(8,128)}) %all-reduce.14.cloned.1.call-update) | async-done | bytes 131088 | tf_op jit(solution)/shard_map/psum | solution.py:46
  537.9 1.2 fusion.234
  542.9 0.9 convolution_bitcast_fusion.62
  545.5 0.9 convolution_bitcast_fusion.61
  550.7 0.9 convolution_bitcast_fusion.59
  553.3 0.9 convolution_bitcast_fusion.58
  555.9 0.9 convolution_bitcast_fusion.57
  561.5 0.9 convolution_bitcast_fusion.55
  564.1 0.9 convolution_bitcast_fusion.54
  569.3 0.9 convolution_bitcast_fusion.52
  571.9 0.9 convolution_bitcast_fusion.51
  573.0 1.3 fusion.233
  575.8 0.9 convolution_bitcast_fusion.50
  578.4 0.9 convolution_bitcast_fusion.49
  583.5 0.9 convolution_bitcast_fusion.47
  586.1 0.9 convolution_bitcast_fusion.46
  588.7 0.9 convolution_bitcast_fusion.45
  593.9 0.9 convolution_bitcast_fusion.43
  596.5 0.9 convolution_bitcast_fusion.42
  599.1 0.9 convolution_bitcast_fusion.41
  604.3 0.9 convolution_bitcast_fusion.39
  609.4 0.9 convolution_bitcast_fusion.37
  612.0 0.9 convolution_bitcast_fusion.36
  622.4 13.9 %fusion.298 = f32[32,4096]{1,0:T(8,128)} fusion(f32[32,1024]{1,0:T(8,128)S(1)} %scatter.425, f32[1024,4096]{1,0:T(8,128)} %copy-done.1), kind=kOutput, calls=%fused_computation.591 | convolution fusion | flops 1610612736 | bytes 17432576 | tf_op jit(solution)/shard_map/dot_general | solution.py:48
  636.5 128.1 %all-reduce.16.cloned.1.call-done = f32[32,4096]{1,0:T(8,128)} async-done(((f32[32,4096]{1,0:T(8,128)}), f32[32,4096]{1,0:T(8,128)}) %all-reduce.16.cloned.1.call-update) | async-done | bytes 524304 | tf_op jit(solution)/shard_map/psum | solution.py:52
  764.6 19.3 %fusion.1 = f32[32,1024]{1,0:T(8,128)} fusion(f32[1024,4096]{1,0:T(8,128)} %copy-done.1, f32[32,4096]{1,0:T(8,128)} %all-reduce.16.cloned.1.call-done), kind=kOutput, calls=%fused_computation.101 | convolution fusion | flops 1610743808 | bytes 17432576 | tf_op jit(solution)/shard_map/dot_general | solution.py:39
  784.0 123.6 %all-reduce.18.cloned.1.call-done = f32[32,1024]{1,0:T(8,128)} async-done(((f32[32,1024]{1,0:T(8,128)}), f32[32,1024]{1,0:T(8,128)}) %all-reduce.18.cloned.1.call-update) | async-done | bytes 131088 | tf_op jit(solution)/shard_map/psum | solution.py:46
  908.6 1.2 fusion.232
  943.3 1.3 fusion.231
  992.7 14.1 %fusion.329 = f32[32,4096]{1,0:T(8,128)} fusion(f32[32,1024]{1,0:T(8,128)S(1)} %scatter.479, f32[1024,4096]{1,0:T(8,128)} %copy-done.1), kind=kOutput, calls=%fused_computation.622 | convolution fusion | flops 1610612736 | bytes 17432576 | tf_op jit(solution)/shard_map/dot_general | solution.py:48
  1006.8 128.3 %all-reduce.20.cloned.1.call-done = f32[32,4096]{1,0:T(8,128)} async-done(((f32[32,4096]{1,0:T(8,128)}), f32[32,4096]{1,0:T(8,128)}) %all-reduce.20.cloned.1.call-update) | async-done | bytes 524304 | tf_op jit(solution)/shard_map/psum | solution.py:54
  1135.0 1.1 broadcast_multiply_fusion
  1136.1 13.6 %fusion.330 = f32[1024,4096]{1,0:T(8,128)S(1)} fusion(f32[32,1024]{1,0:T(8,128)S(1)} %scatter.479, f32[32,4096]{1,0:T(8,128)S(1)} %broadcast_multiply_fusion), kind=kOutput, calls=%fused_computation.623 | convolution fusion | flops 1610612736 | bytes 17432576 | tf_op jit(solution)/shard_map/dot_general | solution.py:20
  1149.7 9.6 fusion
  (461 shorter events, 143.8 us)
Async XLA Ops:
  7.2 1.2 copy-start
  7.2 15.7 %copy-start.3 = (f32[32,4096]{1,0:T(8,128)S(1)}, f32[32,4096]{1,0:T(8,128)}, u32[]{:S(2)}) copy-start(f32[32,4096]{1,0:T(8,128)} %param.200) | copy-start | bytes 1572868
  7.2 159.1 %all-reduce.10.cloned.1.call-start = ((), (), s32[]{:S(2)}) async-start(), calls=%async_computation | async-start | bytes 262144 | tf_op jit(solution)/shard_map/psum | solution.py:46
  17.2 5.7 copy-start.1
  38.9 354.9 %all-reduce.12.cloned.1.call-start = ((), (), s32[]{:S(2)}) async-start(), calls=%async_computation.1 | async-start | bytes 1048576 | tf_op jit(solution)/shard_map/psum | solution.py:52
  265.5 271.2 %all-reduce.14.cloned.1.call-start = ((), (), s32[]{:S(2)}) async-start(), calls=%async_computation.2 | async-start | bytes 262144 | tf_op jit(solution)/shard_map/psum | solution.py:46
  413.1 351.5 %all-reduce.16.cloned.1.call-start = ((), (), s32[]{:S(2)}) async-start(), calls=%async_computation.3 | async-start | bytes 1048576 | tf_op jit(solution)/shard_map/psum | solution.py:52
  636.3 271.2 %all-reduce.18.cloned.1.call-start = ((), (), s32[]{:S(2)}) async-start(), calls=%async_computation.4 | async-start | bytes 262144 | tf_op jit(solution)/shard_map/psum | solution.py:46
  783.9 351.1 %all-reduce.20.cloned.1.call-start = ((), (), s32[]{:S(2)}) async-start(), calls=%async_computation.5 | async-start | bytes 1048576 | tf_op jit(solution)/shard_map/psum | solution.py:54
  1136.1 23.2 %copy-start.2 = (f32[32,4096]{1,0:T(8,128)}, f32[32,4096]{1,0:T(8,128)S(1)}, u32[]{:S(2)}) copy-start(f32[32,4096]{1,0:T(8,128)S(1)} %broadcast_multiply_fusion) | copy-start | bytes 1572868
  1149.7 9.6 copy-start.4
Sparse Core Ops, SparseCore 0:
  39.0 127.2 all-reduce.9
  265.7 128.1 all-reduce.11
  413.3 123.4 all-reduce.13
  636.4 128.1 all-reduce.15
  784.0 123.4 all-reduce.17
  1006.9 128.0 all-reduce.19
where the time goes:
time: 1180 us; the launch traced here: 1170 us
  waiting for transfers between devices  759 us (64%)
  matrix products  229 us (19%)
  between operations  83.2 us (7%)
  other arithmetic  69.8 us (6%)
  local copies, waits for them, and re-layouts  25.2 us (2%)
    psum x3, waiting for transfers between devices, shards(): factor = lax.psum(local_q, 'rep') / count  385 us
    psum x3, waiting for transfers between devices, shards(): total_p = lax.psum(local_p, 'rep')  374 us
    dot_general x96, matrix products, orthonormal(): coef = jnp.dot(basis, vector, precision=lax.Precision.HIGHEST)  89.7 us
    reduce_sum x96, other arithmetic, orthonormal(): basis = basis.at[k].set(vector / jnp.sqrt(jnp.sum(vector * vector) + 1.0))  57.8 us
    dot_general x3, matrix products, shards(): lax.dot_general(factor, merged, (((1,), (1,)), ((), ())), precision=lax.P...  54.5 us
    dot_general x3, matrix products, shards(): jnp.dot(basis, merged, precision=lax.Precision.HIGHEST, preferred_element...  41.9 us
  transfers between devices with their start and end apart: 6, of which 6 were waited for; matrix products, arithmetic and copies ran while one was open for 0% of the time, Pallas kernels for 0%

commit v1 on v0

--- a/solution.py
+++ b/solution.py
@@ -43,7 +43,8 @@
             precision=lax.Precision.HIGHEST,
             preferred_element_type=jnp.float32,
         )
-        total_p = lax.psum(local_p, "rep")
+        parts = lax.all_gather(local_p, "rep", axis=0, tiled=False)
+        total_p = parts.sum(axis=0)
         basis = orthonormal(total_p)
         local_q = jnp.dot(
             basis, merged, precision=lax.Precision.HIGHEST, preferred_element_type=jnp.float32

time: 1180 us -> 984 us (0.83)
  waiting for transfers between devices: 759 us -> 570 us
    psum x3 -> x0, waiting for transfers between devices: 374 us -> none  [shards(): total_p = lax.psum(local_p, 'rep')]
    all_gather x0 -> x3, waiting for transfers between devices: none -> 186 us  [shards(): parts = lax.all_gather(local_p, 'rep', axis=0, tiled=False)]
where the time goes in v1:
time: 984 us; the launch traced here: 974 us
  waiting for transfers between devices  570 us (58%)
  matrix products  225 us (23%)
  between operations  83.3 us (8%)
  other arithmetic  77.1 us (8%)
  local copies, waits for them, and re-layouts  18.2 us (2%)
    psum x3, waiting for transfers between devices, shards(): factor = lax.psum(local_q, 'rep') / count  384 us
    all_gather x3, waiting for transfers between devices, shards(): parts = lax.all_gather(local_p, 'rep', axis=0, tiled=False)  186 us
    dot_general x96, matrix products, orthonormal(): coef = jnp.dot(basis, vector, precision=lax.Precision.HIGHEST)  85.3 us
    reduce_sum x96, other arithmetic, orthonormal(): basis = basis.at[k].set(vector / jnp.sqrt(jnp.sum(vector * vector) + 1.0))  57.8 us
    dot_general x3, matrix products, shards(): lax.dot_general(factor, merged, (((1,), (1,)), ((), ())), precision=lax.P...  54.5 us
    dot_general x3, matrix products, shards(): jnp.dot(basis, merged, precision=lax.Precision.HIGHEST, preferred_element...  41.7 us
    dot_general x96, matrix products, orthonormal(): vector = vector - jnp.dot(coef, basis, precision=lax.Precision.HIGHEST)  20.9 us
  transfers between devices with their start and end apart: 6, of which 6 were waited for; matrix products, arithmetic and copies ran while one was open for 0% of the time, Pallas kernels for 0%

profile of v1, /device:TPU:0, one launch (start us, length us, event | category | flops | bytes accessed | tf_op | source)
XLA Modules:
  0.0 974.0 jit_solution(2108467096827677061)
XLA Ops:
  7.2 1.2 copy-done
  8.4 8.8 convert_add_fusion
  17.2 5.7 copy-done.2
  22.9 16.0 %convolution_bitcast_fusion = f32[32,1024]{1,0:T(8,128)} fusion(f32[1024,4096]{1,0:T(8,128)S(1)} %convert_add_fusion, f32[32,4096]{1,0:T(8,128)S(1)} %copy-done.7), kind=kOutput, calls=%fused_computation.3 | convolution fusion | flops 1610612736 | bytes 17432576 | tf_op jit(solution)/shard_map/dot_general | solution.py:39
  39.1 64.4 %all-gather.7.cloned.1.call-done = f32[1024,1024]{1,0:T(8,128)} async-done(((f32[32,1024]{1,0:T(8,128)}), f32[1024,1024]{1,0:T(8,128)}) %all-gather.7.cloned.1.call-update) | async-done | bytes 4194320 | tf_op jit(solution)/shard_map/all_gather | solution.py:46
  103.5 2.4 reduce_sum.891
  127.6 0.9 convolution_bitcast_fusion.87
  130.2 0.9 convolution_bitcast_fusion.86
  132.8 0.9 convolution_bitcast_fusion.85
  135.4 0.9 convolution_bitcast_fusion.84
  138.0 0.9 convolution_bitcast_fusion.83
  140.6 0.9 convolution_bitcast_fusion.82
  143.2 0.9 convolution_bitcast_fusion.81
  148.4 0.9 convolution_bitcast_fusion.79
  150.9 0.9 convolution_bitcast_fusion.78
  153.5 0.9 convolution_bitcast_fusion.77
  156.1 0.9 convolution_bitcast_fusion.76
  158.7 0.9 convolution_bitcast_fusion.75
  161.3 0.9 convolution_bitcast_fusion.74
  163.9 0.9 convolution_bitcast_fusion.73
  169.1 0.9 convolution_bitcast_fusion.71
  171.7 0.9 convolution_bitcast_fusion.70
  174.3 0.9 convolution_bitcast_fusion.69
  176.9 0.9 convolution_bitcast_fusion.68
  179.4 0.9 convolution_bitcast_fusion.67
  182.0 0.9 convolution_bitcast_fusion.66
  184.6 0.9 convolution_bitcast_fusion.65
  187.4 13.9 %fusion.267 = f32[32,4096]{1,0:T(8,128)} fusion(f32[32,1024]{1,0:T(8,128)S(1)} %scatter.371, f32[1024,4096]{1,0:T(8,128)} %copy-done.2), kind=kOutput, calls=%fused_computation.560 | convolution fusion | flops 1610612736 | bytes 17432576 | tf_op jit(solution)/shard_map/dot_general | solution.py:49
  201.4 128.0 %all-reduce.7.cloned.1.call-done = f32[32,4096]{1,0:T(8,128)} async-done(((f32[32,4096]{1,0:T(8,128)}), f32[32,4096]{1,0:T(8,128)}) %all-reduce.7.cloned.1.call-update) | async-done | bytes 524304 | tf_op jit(solution)/shard_map/psum | solution.py:53
  329.4 19.3 %fusion.3 = f32[32,1024]{1,0:T(8,128)} fusion(f32[1024,4096]{1,0:T(8,128)} %copy-done.2, f32[32,4096]{1,0:T(8,128)} %all-reduce.7.cloned.1.call-done), kind=kOutput, calls=%fused_computation.103 | convolution fusion | flops 1610743808 | bytes 17432576 | tf_op jit(solution)/shard_map/dot_general | solution.py:39
  348.7 60.9 %all-gather.9.cloned.1.call-done = f32[1024,1024]{1,0:T(8,128)} async-done(((f32[32,1024]{1,0:T(8,128)}), f32[1024,1024]{1,0:T(8,128)}) %all-gather.9.cloned.1.call-update) | async-done | bytes 4194320 | tf_op jit(solution)/shard_map/all_gather | solution.py:46
  409.6 2.4 reduce_sum.924
  434.1 0.9 convolution_bitcast_fusion.55
  436.7 0.9 convolution_bitcast_fusion.54
  439.3 0.9 convolution_bitcast_fusion.53
  441.9 0.9 convolution_bitcast_fusion.52
  444.5 0.9 convolution_bitcast_fusion.51
  447.1 0.9 convolution_bitcast_fusion.50
  449.7 0.9 convolution_bitcast_fusion.49
  454.9 0.9 convolution_bitcast_fusion.47
  457.4 0.9 convolution_bitcast_fusion.46
  460.0 0.9 convolution_bitcast_fusion.45
  462.6 0.9 convolution_bitcast_fusion.44
  465.2 0.9 convolution_bitcast_fusion.43
  467.8 0.9 convolution_bitcast_fusion.42
  470.4 0.9 convolution_bitcast_fusion.41
  475.6 0.9 convolution_bitcast_fusion.39
  478.2 0.9 convolution_bitcast_fusion.38
  480.8 0.9 convolution_bitcast_fusion.37
  483.3 0.9 convolution_bitcast_fusion.36
  485.9 0.9 convolution_bitcast_fusion.35
  488.5 0.9 convolution_bitcast_fusion.34
  491.1 0.9 convolution_bitcast_fusion.33
  493.7 13.9 %fusion.298 = f32[32,4096]{1,0:T(8,128)} fusion(f32[32,1024]{1,0:T(8,128)S(1)} %scatter.425, f32[1024,4096]{1,0:T(8,128)} %copy-done.2), kind=kOutput, calls=%fused_computation.591 | convolution fusion | flops 1610612736 | bytes 17432576 | tf_op jit(solution)/shard_map/dot_general | solution.py:49
  507.9 127.8 %all-reduce.9.cloned.1.call-done = f32[32,4096]{1,0:T(8,128)} async-done(((f32[32,4096]{1,0:T(8,128)}), f32[32,4096]{1,0:T(8,128)}) %all-reduce.9.cloned.1.call-update) | async-done | bytes 524304 | tf_op jit(solution)/shard_map/psum | solution.py:53
  635.6 19.3 %fusion.1 = f32[32,1024]{1,0:T(8,128)} fusion(f32[1024,4096]{1,0:T(8,128)} %copy-done.2, f32[32,4096]{1,0:T(8,128)} %all-reduce.9.cloned.1.call-done), kind=kOutput, calls=%fused_computation.101 | convolution fusion | flops 1610743808 | bytes 17432576 | tf_op jit(solution)/shard_map/dot_general | solution.py:39
  655.0 60.9 %all-gather.11.cloned.1.call-done = f32[1024,1024]{1,0:T(8,128)} async-done(((f32[32,1024]{1,0:T(8,128)}), f32[1024,1024]{1,0:T(8,128)}) %all-gather.11.cloned.1.call-update) | async-done | bytes 4194320 | tf_op jit(solution)/shard_map/all_gather | solution.py:46
  715.9 2.4 reduce_sum.957
  786.9 0.9 convolution_bitcast_fusion.5
  799.8 13.9 %fusion.329 = f32[32,4096]{1,0:T(8,128)} fusion(f32[32,1024]{1,0:T(8,128)S(1)} %scatter.479, f32[1024,4096]{1,0:T(8,128)} %copy-done.2), kind=kOutput, calls=%fused_computation.622 | convolution fusion | flops 1610612736 | bytes 17432576 | tf_op jit(solution)/shard_map/dot_general | solution.py:49
  813.7 128.0 %all-reduce.11.cloned.1.call-done = f32[32,4096]{1,0:T(8,128)} async-done(((f32[32,4096]{1,0:T(8,128)}), f32[32,4096]{1,0:T(8,128)}) %all-reduce.11.cloned.1.call-update) | async-done | bytes 524304 | tf_op jit(solution)/shard_map/psum | solution.py:55
  941.8 1.1 broadcast_multiply_fusion
  942.9 13.6 %fusion.330 = f32[1024,4096]{1,0:T(8,128)S(1)} fusion(f32[32,1024]{1,0:T(8,128)S(1)} %scatter.479, f32[32,4096]{1,0:T(8,128)S(1)} %broadcast_multiply_fusion), kind=kOutput, calls=%fused_computation.623 | convolution fusion | flops 1610612736 | bytes 17432576 | tf_op jit(solution)/shard_map/dot_general | solution.py:20
  956.5 9.6 fusion
  (472 shorter events, 137.1 us)
Async XLA Ops:
  7.2 1.2 copy-start
  7.2 15.7 %copy-start.7 = (f32[32,4096]{1,0:T(8,128)S(1)}, f32[32,4096]{1,0:T(8,128)}, u32[]{:S(2)}) copy-start(f32[32,4096]{1,0:T(8,128)} %param.200) | copy-start | bytes 1572868
  7.2 96.3 %all-gather.7.cloned.1.call-start = ((), (), s32[]{:S(2)}) async-start(), calls=%async_computation.3 | async-start | bytes 4325376 | tf_op jit(solution)/shard_map/all_gather | solution.py:46
  17.2 5.7 copy-start.2
  38.9 290.5 %all-reduce.7.cloned.1.call-start = ((), (), s32[]{:S(2)}) async-start(), calls=%async_computation | async-start | bytes 1048576 | tf_op jit(solution)/shard_map/psum | solution.py:53
  105.9 3.6 copy-start.4
  201.4 208.2 %all-gather.9.cloned.1.call-start = ((), (), s32[]{:S(2)}) async-start(), calls=%async_computation.4 | async-start | bytes 4325376 | tf_op jit(solution)/shard_map/all_gather | solution.py:46
  348.7 287.0 %all-reduce.9.cloned.1.call-start = ((), (), s32[]{:S(2)}) async-start(), calls=%async_computation.1 | async-start | bytes 1048576 | tf_op jit(solution)/shard_map/psum | solution.py:53
  412.0 3.6 copy-start.5
  507.6 208.2 %all-gather.11.cloned.1.call-start = ((), (), s32[]{:S(2)}) async-start(), calls=%async_computation.5 | async-start | bytes 4325376 | tf_op jit(solution)/shard_map/all_gather | solution.py:46
  655.0 286.8 %all-reduce.11.cloned.1.call-start = ((), (), s32[]{:S(2)}) async-start(), calls=%async_computation.2 | async-start | bytes 1048576 | tf_op jit(solution)/shard_map/psum | solution.py:55
  718.3 3.6 copy-start.3
  942.8 23.2 %copy-start.6 = (f32[32,4096]{1,0:T(8,128)}, f32[32,4096]{1,0:T(8,128)S(1)}, u32[]{:S(2)}) copy-start(f32[32,4096]{1,0:T(8,128)S(1)} %broadcast_multiply_fusion) | copy-start | bytes 1572868
  942.8 24.1 %copy-start.1 = (bf16[512,1024]{1,0:T(8,128)(2,1)S(1)}, bf16[512,1024]{1,0:T(8,128)(2,1)}, u32[]{:S(2)}) copy-start(bf16[512,1024]{1,0:T(8,128)(2,1)} %param.197) | copy-start | bytes 3145732
  956.5 9.6 copy-start.8
Sparse Core Ops, SparseCore 0:
  39.0 64.4 all-gather.6
  201.5 127.8 all-reduce.6
  348.8 60.7 all-gather.8
  507.8 127.8 all-reduce.8
  655.1 60.7 all-gather.10
  813.9 127.8 all-reduce.10
